TPU v7x, 32 devices: a whole 2x2x4 slice. The times are simulated.
32 devices in a mesh: row: 8 (over y, x, core), col: 4 (over z).
Axes of the slice: x: 2, y: 2, z: 4, core: 2. Of those that a mesh axis runs over, the one named last changes fastest.
Arguments:
- front_tiles: float32 [2, 2048, 2, 1024], P(None, 'row', None, 'col'), may hold values from -6 to 6, as said below
- lead_tiles: int32 [2, 8], P(None, 'row'), may hold values from 0 to 7
- damping: float32 [2, 1024], P(None, 'col'), may hold values from 1.5 to 6
Outputs:
- factor: float32 [2, 2048, 2, 1024], P(None, 'row', None, 'col')
Inputs may be any that keep to these rules, and one draw needn't show every extreme that they name: `front_tiles`: the front's entries. `lead_tiles`: entries of the first 8 tile rows are not read.
All inputs are finite; a program needn't handle non-finite values.
Results may differ from a plain program's by a relative error of at most 0.00005.
Values sent between devices are 32-bit elements; how exact they have to be, the bound alone decides.
No kernel may reach another device: no remote copies, remote signals or barrier semaphores. Data moves between devices by JAX's collectives and lax.ppermute only.
A program may use at most 64 MiB of HBM per device.

v0:
```python
import jax
import jax.numpy as jnp
from jax import lax
from jax.sharding import PartitionSpec as P


def from_root(value, axis, source):
    kept = jnp.where(lax.axis_index(axis) == source, value, 0).astype(value.dtype)
    return lax.psum(kept, axis)


def pick_tile(tiles, tile_rows, wanted):
    chosen = (tile_rows == wanted)[:, None, None]
    return jnp.sum(jnp.where(chosen, tiles, 0.0), axis=0)


def shards(front_tiles, lead_tiles, damping):
    slot_count, tile_size, col_slot_count, _ = front_tiles.shape
    n_row = lax.axis_size("row")
    n_col = lax.axis_size("col")
    row_at = lax.axis_index("row")
    col_at = lax.axis_index("col")
    n_columns = col_slot_count * n_col
    row_tiles = jnp.arange(slot_count, dtype=jnp.int32) * n_row + row_at
    col_tiles = jnp.arange(col_slot_count, dtype=jnp.int32) * n_col + col_at
    leads = jnp.where(row_tiles < n_columns, 0, lead_tiles[:, 0])
    working = front_tiles
    kept_mask = col_tiles[None, :] >= leads[:, None]
    working = jnp.where(kept_mask[:, None, :, None], working, 0.0)
    identity = jnp.eye(tile_size, dtype=jnp.float32)
    on_diagonal = (row_tiles[:, None] == col_tiles[None, :])[:, None, :, None]
    damp_term = identity[None, :, None, :] * damping[None, None, :, :]
    working = working + jnp.where(on_diagonal, damp_term, 0.0)
    for column in range(n_columns):
        owner_col = column % n_col
        col_slot = column // n_col
        column_panel = working[:, :, col_slot, :]
        diag_source = pick_tile(column_panel, row_tiles, column)
        diag_full = from_root(diag_source, "row", column % n_row)
        symmetric = jnp.tril(diag_full) + jnp.tril(diag_full, -1).T
        lower_factor = jnp.linalg.cholesky(symmetric)
        flattened = column_panel.reshape(slot_count * tile_size, tile_size)
        solved = jax.scipy.linalg.solve_triangular(lower_factor, flattened.T, lower=True).T
        solved = solved.reshape(slot_count, tile_size, tile_size)
        below = (row_tiles > column)[:, None, None]
        at_diag = (row_tiles == column)[:, None, None]
        new_panel = jnp.where(below, solved, jnp.where(at_diag, lower_factor[None], 0.0))
        is_owner = col_at == owner_col
        working = working.at[:, :, col_slot, :].set(jnp.where(is_owner, new_panel, column_panel))
        shared = from_root(new_panel, "col", owner_col)
        for target_slot in range(col_slot_count):
            target = col_tiles[target_slot]
            sep_source = pick_tile(shared, row_tiles, target)
            sep_tile = from_root(sep_source, "row", target)

            def apply_all(current):
                product_update = jnp.dot(
                    shared.reshape(slot_count * tile_size, tile_size),
                    sep_tile.T,
                    precision=lax.Precision.HIGHEST,
                    preferred_element_type=jnp.float32,
                )
                return current - product_update.reshape(slot_count, tile_size, tile_size)

            def keep_same(current):
                return current

            updated = lax.cond(target > column, apply_all, keep_same, working[:, :, target_slot, :])
            working = working.at[:, :, target_slot, :].set(updated)
    final_mask = kept_mask & (row_tiles[:, None] >= col_tiles[None, :])
    result = jnp.where(final_mask[:, None, :, None], working, 0.0)
    return result


def solution(mesh):
    in_specs = (P(None, "row", None, "col"), P(None, "row"), P(None, "col"))
    out_specs = P(None, "row", None, "col")
    return jax.shard_map(shards, mesh=mesh, in_specs=in_specs, out_specs=out_specs, check_vma=False)
```

profile of v0, /device:TPU:0, one launch (start us, length us, event | category | flops | bytes accessed | tf_op | source)
XLA Modules:
  0.0 1757.5 jit_solution(1839295650670124243)
XLA Ops:
  9.5 57.1 %all-reduce.34.cloned.1.call-done = f32[256,256]{1,0:T(8,128)} async-done(((f32[256,256]{1,0:T(8,128)}), f32[256,256]{1,0:T(8,128)}) %all-reduce.34.cloned.1.call-update) | async-done | bytes 262160 | tf_op jit(solution)/shard_map/psum | solution.py:9
  68.2 11.7 cholesky.382
  80.0 9.8 custom-call.25
  90.4 11.7 cholesky.399
  104.4 4.6 while.40
  109.0 19.7 %custom-call.26 = f32[2,128,128]{1,2,0:T(8,128)S(1)} custom-call(f32[2,128,128]{2,1,0:T(8,128)S(1)} %get-tuple-element.649), custom_call_target="InvertDiagBlocksLowerTriangular" | custom-call | tf_op jit(solution)/shard_map/jit(_solve_triangular)/triangular_solve | solution.py:43
  135.7 33.3 %all-reduce.36.cloned.1.call-done = f32[2,256,256]{2,1,0:T(8,128)} async-done(((f32[2,256,256]{2,1,0:T(8,128)}), f32[2,256,256]{2,1,0:T(8,128)}) %all-reduce.36.cloned.1.call-update) | async-done | bytes 524304 | tf_op jit(solution)/shard_map/psum | solution.py:9
  171.9 55.2 %all-reduce.80.cloned.1.call-done = (f32[256,256]{1,0:T(8,128)}, f32[256,256]{1,0:T(8,128)}) async-done(((f32[256,256]{1,0:T(8,128)}, f32[256,256]{1,0:T(8,128)}), (f32[256,256]{1,0:T(8,128)}, f32[256,256]{1,0:T(8,128)})) %all-reduce.80.cloned.1.call-update) | async-done | bytes 524304 | tf_op jit(solution)/shard_map/psum | solution.py:9
  230.1 54.3 %all-reduce.38.cloned.1.call-done = f32[256,256]{1,0:T(8,128)} async-done(((f32[256,256]{1,0:T(8,128)}), f32[256,256]{1,0:T(8,128)}) %all-reduce.38.cloned.1.call-update) | async-done | bytes 262160 | tf_op jit(solution)/shard_map/psum | solution.py:9
  285.9 11.7 cholesky.416
  297.7 9.8 custom-call.27
  308.2 11.7 cholesky.433
  322.7 4.3 while.41
  327.0 19.7 %custom-call.28 = f32[2,128,128]{1,2,0:T(8,128)S(1)} custom-call(f32[2,128,128]{2,1,0:T(8,128)S(1)} %get-tuple-element.650), custom_call_target="InvertDiagBlocksLowerTriangular" | custom-call | tf_op jit(solution)/shard_map/jit(_solve_triangular)/triangular_solve | solution.py:43
  350.5 36.5 %all-reduce.40.cloned.1.call-done = f32[2,256,256]{2,1,0:T(8,128)} async-done(((f32[2,256,256]{2,1,0:T(8,128)}), f32[2,256,256]{2,1,0:T(8,128)}) %all-reduce.40.cloned.1.call-update) | async-done | bytes 524304 | tf_op jit(solution)/shard_map/psum | solution.py:9
  390.0 55.0 %all-reduce.78.cloned.1.call-done = (f32[256,256]{1,0:T(8,128)}, f32[256,256]{1,0:T(8,128)}) async-done(((f32[256,256]{1,0:T(8,128)}, f32[256,256]{1,0:T(8,128)}), (f32[256,256]{1,0:T(8,128)}, f32[256,256]{1,0:T(8,128)})) %all-reduce.78.cloned.1.call-update) | async-done | bytes 524304 | tf_op jit(solution)/shard_map/psum | solution.py:9
  448.0 54.3 %all-reduce.42.cloned.1.call-done = f32[256,256]{1,0:T(8,128)} async-done(((f32[256,256]{1,0:T(8,128)}), f32[256,256]{1,0:T(8,128)}) %all-reduce.42.cloned.1.call-update) | async-done | bytes 262160 | tf_op jit(solution)/shard_map/psum | solution.py:9
  503.8 11.7 cholesky.450
  515.6 9.8 custom-call.29
  526.1 11.7 cholesky.467
  540.6 4.5 while.42
  545.1 19.7 %custom-call.30 = f32[2,128,128]{1,2,0:T(8,128)S(1)} custom-call(f32[2,128,128]{2,1,0:T(8,128)S(1)} %get-tuple-element.651), custom_call_target="InvertDiagBlocksLowerTriangular" | custom-call | tf_op jit(solution)/shard_map/jit(_solve_triangular)/triangular_solve | solution.py:43
  568.6 36.5 %all-reduce.44.cloned.1.call-done = f32[2,256,256]{2,1,0:T(8,128)} async-done(((f32[2,256,256]{2,1,0:T(8,128)}), f32[2,256,256]{2,1,0:T(8,128)}) %all-reduce.44.cloned.1.call-update) | async-done | bytes 524304 | tf_op jit(solution)/shard_map/psum | solution.py:9
  608.1 55.2 %all-reduce.76.cloned.1.call-done = (f32[256,256]{1,0:T(8,128)}, f32[256,256]{1,0:T(8,128)}) async-done(((f32[256,256]{1,0:T(8,128)}, f32[256,256]{1,0:T(8,128)}), (f32[256,256]{1,0:T(8,128)}, f32[256,256]{1,0:T(8,128)})) %all-reduce.76.cloned.1.call-update) | async-done | bytes 524304 | tf_op jit(solution)/shard_map/psum | solution.py:9
  666.2 54.4 %all-reduce.46.cloned.1.call-done = f32[256,256]{1,0:T(8,128)} async-done(((f32[256,256]{1,0:T(8,128)}), f32[256,256]{1,0:T(8,128)}) %all-reduce.46.cloned.1.call-update) | async-done | bytes 262160 | tf_op jit(solution)/shard_map/psum | solution.py:9
  722.1 11.7 cholesky.484
  733.9 9.8 custom-call.31
  744.3 11.7 cholesky.501
  758.8 4.3 while.43
  763.1 19.7 %custom-call.32 = f32[2,128,128]{1,2,0:T(8,128)S(1)} custom-call(f32[2,128,128]{2,1,0:T(8,128)S(1)} %get-tuple-element.652), custom_call_target="InvertDiagBlocksLowerTriangular" | custom-call | tf_op jit(solution)/shard_map/jit(_solve_triangular)/triangular_solve | solution.py:43
  786.7 36.4 %all-reduce.48.cloned.1.call-done = f32[2,256,256]{2,1,0:T(8,128)} async-done(((f32[2,256,256]{2,1,0:T(8,128)}), f32[2,256,256]{2,1,0:T(8,128)}) %all-reduce.48.cloned.1.call-update) | async-done | bytes 524304 | tf_op jit(solution)/shard_map/psum | solution.py:9
  826.1 55.0 %all-reduce.74.cloned.1.call-done = (f32[256,256]{1,0:T(8,128)}, f32[256,256]{1,0:T(8,128)}) async-done(((f32[256,256]{1,0:T(8,128)}, f32[256,256]{1,0:T(8,128)}), (f32[256,256]{1,0:T(8,128)}, f32[256,256]{1,0:T(8,128)})) %all-reduce.74.cloned.1.call-update) | async-done | bytes 524304 | tf_op jit(solution)/shard_map/psum | solution.py:9
  884.0 53.0 %all-reduce.50.cloned.1.call-done = f32[256,256]{1,0:T(8,128)} async-done(((f32[256,256]{1,0:T(8,128)}), f32[256,256]{1,0:T(8,128)}) %all-reduce.50.cloned.1.call-update) | async-done | bytes 262160 | tf_op jit(solution)/shard_map/psum | solution.py:9
  938.5 11.7 cholesky.518
  950.3 9.8 custom-call.33
  960.7 11.7 cholesky.535
  975.2 4.5 while.44
  979.8 19.7 %custom-call.34 = f32[2,128,128]{1,2,0:T(8,128)S(1)} custom-call(f32[2,128,128]{2,1,0:T(8,128)S(1)} %get-tuple-element.653), custom_call_target="InvertDiagBlocksLowerTriangular" | custom-call | tf_op jit(solution)/shard_map/jit(_solve_triangular)/triangular_solve | solution.py:43
  1003.3 36.4 %all-reduce.52.cloned.1.call-done = f32[2,256,256]{2,1,0:T(8,128)} async-done(((f32[2,256,256]{2,1,0:T(8,128)}), f32[2,256,256]{2,1,0:T(8,128)}) %all-reduce.52.cloned.1.call-update) | async-done | bytes 524304 | tf_op jit(solution)/shard_map/psum | solution.py:9
  1042.7 55.0 %all-reduce.72.cloned.1.call-done = (f32[256,256]{1,0:T(8,128)}, f32[256,256]{1,0:T(8,128)}) async-done(((f32[256,256]{1,0:T(8,128)}, f32[256,256]{1,0:T(8,128)}), (f32[256,256]{1,0:T(8,128)}, f32[256,256]{1,0:T(8,128)})) %all-reduce.72.cloned.1.call-update) | async-done | bytes 524304 | tf_op jit(solution)/shard_map/psum | solution.py:9
  1099.8 53.6 %all-reduce.54.cloned.1.call-done = f32[256,256]{1,0:T(8,128)} async-done(((f32[256,256]{1,0:T(8,128)}), f32[256,256]{1,0:T(8,128)}) %all-reduce.54.cloned.1.call-update) | async-done | bytes 262160 | tf_op jit(solution)/shard_map/psum | solution.py:9
  1154.9 11.7 cholesky.552
  1166.7 9.8 custom-call.35
  1177.2 11.7 cholesky.569
  1191.7 4.3 while.45
  1196.0 19.7 %custom-call.36 = f32[2,128,128]{1,2,0:T(8,128)S(1)} custom-call(f32[2,128,128]{2,1,0:T(8,128)S(1)} %get-tuple-element.654), custom_call_target="InvertDiagBlocksLowerTriangular" | custom-call | tf_op jit(solution)/shard_map/jit(_solve_triangular)/triangular_solve | solution.py:43
  1219.5 36.4 %all-reduce.56.cloned.1.call-done = f32[2,256,256]{2,1,0:T(8,128)} async-done(((f32[2,256,256]{2,1,0:T(8,128)}), f32[2,256,256]{2,1,0:T(8,128)}) %all-reduce.56.cloned.1.call-update) | async-done | bytes 524304 | tf_op jit(solution)/shard_map/psum | solution.py:9
  1258.9 55.0 %all-reduce.70.cloned.1.call-done = (f32[256,256]{1,0:T(8,128)}, f32[256,256]{1,0:T(8,128)}) async-done(((f32[256,256]{1,0:T(8,128)}, f32[256,256]{1,0:T(8,128)}), (f32[256,256]{1,0:T(8,128)}, f32[256,256]{1,0:T(8,128)})) %all-reduce.70.cloned.1.call-update) | async-done | bytes 524304 | tf_op jit(solution)/shard_map/psum | solution.py:9
  1316.2 53.6 %all-reduce.58.cloned.1.call-done = f32[256,256]{0,1:T(8,128)} async-done(((f32[256,256]{0,1:T(8,128)}), f32[256,256]{0,1:T(8,128)}) %all-reduce.58.cloned.1.call-update) | async-done | bytes 262160 | tf_op jit(solution)/shard_map/psum | solution.py:9
  1371.3 11.7 cholesky.586
  1383.1 9.8 custom-call.37
  1393.6 11.7 cholesky.603
  1408.1 4.5 while.46
  1412.6 19.7 %custom-call.38 = f32[2,128,128]{1,2,0:T(8,128)S(1)} custom-call(f32[2,128,128]{2,1,0:T(8,128)S(1)} %get-tuple-element.655), custom_call_target="InvertDiagBlocksLowerTriangular" | custom-call | tf_op jit(solution)/shard_map/jit(_solve_triangular)/triangular_solve | solution.py:43
  1436.1 36.4 %all-reduce.60.cloned.1.call-done = f32[2,256,256]{2,1,0:T(8,128)} async-done(((f32[2,256,256]{2,1,0:T(8,128)}), f32[2,256,256]{2,1,0:T(8,128)}) %all-reduce.60.cloned.1.call-update) | async-done | bytes 524304 | tf_op jit(solution)/shard_map/psum | solution.py:9
  1475.5 55.1 %all-reduce.68.cloned.1.call-done = (f32[256,256]{1,0:T(8,128)}, f32[256,256]{1,0:T(8,128)}) async-done(((f32[256,256]{1,0:T(8,128)}, f32[256,256]{1,0:T(8,128)}), (f32[256,256]{1,0:T(8,128)}, f32[256,256]{1,0:T(8,128)})) %all-reduce.68.cloned.1.call-update) | async-done | bytes 524304 | tf_op jit(solution)/shard_map/psum | solution.py:9
  1533.0 53.5 %all-reduce.62.cloned.1.call-done = f32[256,256]{1,0:T(8,128)} async-done(((f32[256,256]{1,0:T(8,128)}), f32[256,256]{1,0:T(8,128)}) %all-reduce.62.cloned.1.call-update) | async-done | bytes 262160 | tf_op jit(solution)/shard_map/psum | solution.py:9
  1588.7 11.7 cholesky.620
  1600.5 9.8 custom-call.39
  1610.8 11.7 cholesky.637
  1625.3 4.3 while.47
  1629.6 19.7 %custom-call.40 = f32[2,128,128]{1,2,0:T(8,128)S(1)} custom-call(f32[2,128,128]{2,1,0:T(8,128)S(1)} %get-tuple-element.656), custom_call_target="InvertDiagBlocksLowerTriangular" | custom-call | tf_op jit(solution)/shard_map/jit(_solve_triangular)/triangular_solve | solution.py:43
  1653.1 36.4 %all-reduce.64.cloned.1.call-done = f32[2,256,256]{2,1,0:T(8,128)} async-done(((f32[2,256,256]{2,1,0:T(8,128)}), f32[2,256,256]{2,1,0:T(8,128)}) %all-reduce.64.cloned.1.call-update) | async-done | bytes 524304 | tf_op jit(solution)/shard_map/psum | solution.py:9
  1692.5 55.0 %all-reduce.66.cloned.1.call-done = (f32[256,256]{1,0:T(8,128)}, f32[256,256]{1,0:T(8,128)}) async-done(((f32[256,256]{1,0:T(8,128)}, f32[256,256]{1,0:T(8,128)}), (f32[256,256]{1,0:T(8,128)}, f32[256,256]{1,0:T(8,128)})) %all-reduce.66.cloned.1.call-update) | async-done | bytes 524304 | tf_op jit(solution)/shard_map/psum | solution.py:9
  (461 shorter events, 133.3 us)
Async XLA Ops:
  6.5 1.6 copy-start.8
  6.5 60.1 %all-reduce.34.cloned.1.call-start = ((), (), s32[]{:S(2)}) async-start(), calls=%async_computation | async-start | bytes 524288 | tf_op jit(solution)/shard_map/psum | solution.py:9
  9.2 159.8 %all-reduce.36.cloned.1.call-start = ((), (), s32[]{:S(2)}) async-start(), calls=%async_computation.1 | async-start | bytes 1048576 | tf_op jit(solution)/shard_map/psum | solution.py:9
  66.7 1.2 copy-start.10
  131.1 96.0 %all-reduce.80.cloned.1.call-start = ((), (), s32[]{:S(2)}) async-start(), calls=%async_computation.23 | async-start | bytes 1048576 | tf_op jit(solution)/shard_map/psum | solution.py:9
  171.7 112.7 %all-reduce.38.cloned.1.call-start = ((), (), s32[]{:S(2)}) async-start(), calls=%async_computation.2 | async-start | bytes 524288 | tf_op jit(solution)/shard_map/psum | solution.py:9
  171.7 55.4 %copy-start = (f32[2,256,256]{2,1,0:T(8,128)S(1)}, f32[2,256,256]{2,1,0:T(8,128)}, u32[]{:S(2)}) copy-start(f32[2,256,256]{2,1,0:T(8,128)} %all-reduce.36.cloned.1.call-done) | copy-start | bytes 1572868
  227.1 1.0 copy-start.21
  229.8 157.2 %all-reduce.40.cloned.1.call-start = ((), (), s32[]{:S(2)}) async-start(), calls=%async_computation.3 | async-start | bytes 1048576 | tf_op jit(solution)/shard_map/psum | solution.py:9
  284.4 1.2 copy-start.12
  349.1 95.8 %all-reduce.78.cloned.1.call-start = ((), (), s32[]{:S(2)}) async-start(), calls=%async_computation.22 | async-start | bytes 1048576 | tf_op jit(solution)/shard_map/psum | solution.py:9
  389.7 112.6 %all-reduce.42.cloned.1.call-start = ((), (), s32[]{:S(2)}) async-start(), calls=%async_computation.4 | async-start | bytes 524288 | tf_op jit(solution)/shard_map/psum | solution.py:9
  389.8 55.2 %copy-start.7 = (f32[2,256,256]{2,1,0:T(8,128)S(1)}, f32[2,256,256]{2,1,0:T(8,128)}, u32[]{:S(2)}) copy-start(f32[2,256,256]{2,1,0:T(8,128)} %all-reduce.40.cloned.1.call-done) | copy-start | bytes 1572868
  445.0 1.0 copy-start.22
  447.6 157.4 %all-reduce.44.cloned.1.call-start = ((), (), s32[]{:S(2)}) async-start(), calls=%async_computation.5 | async-start | bytes 1048576 | tf_op jit(solution)/shard_map/psum | solution.py:9
  502.3 1.2 copy-start.13
  567.3 96.0 %all-reduce.76.cloned.1.call-start = ((), (), s32[]{:S(2)}) async-start(), calls=%async_computation.21 | async-start | bytes 1048576 | tf_op jit(solution)/shard_map/psum | solution.py:9
  607.8 112.7 %all-reduce.46.cloned.1.call-start = ((), (), s32[]{:S(2)}) async-start(), calls=%async_computation.6 | async-start | bytes 524288 | tf_op jit(solution)/shard_map/psum | solution.py:9
  607.9 55.4 %copy-start.5 = (f32[2,256,256]{2,1,0:T(8,128)S(1)}, f32[2,256,256]{2,1,0:T(8,128)}, u32[]{:S(2)}) copy-start(f32[2,256,256]{2,1,0:T(8,128)} %all-reduce.44.cloned.1.call-done) | copy-start | bytes 1572868
  663.3 1.0 copy-start.23
  665.9 157.2 %all-reduce.48.cloned.1.call-start = ((), (), s32[]{:S(2)}) async-start(), calls=%async_computation.7 | async-start | bytes 1048576 | tf_op jit(solution)/shard_map/psum | solution.py:9
  720.6 1.2 copy-start.11
  785.3 95.8 %all-reduce.74.cloned.1.call-start = ((), (), s32[]{:S(2)}) async-start(), calls=%async_computation.20 | async-start | bytes 1048576 | tf_op jit(solution)/shard_map/psum | solution.py:9
  825.8 111.1 %all-reduce.50.cloned.1.call-start = ((), (), s32[]{:S(2)}) async-start(), calls=%async_computation.8 | async-start | bytes 524288 | tf_op jit(solution)/shard_map/psum | solution.py:9
  825.9 55.2 %copy-start.6 = (f32[2,256,256]{2,1,0:T(8,128)S(1)}, f32[2,256,256]{2,1,0:T(8,128)}, u32[]{:S(2)}) copy-start(f32[2,256,256]{2,1,0:T(8,128)} %all-reduce.48.cloned.1.call-done) | copy-start | bytes 1572868
  881.1 1.0 copy-start.24
  883.7 156.0 %all-reduce.52.cloned.1.call-start = ((), (), s32[]{:S(2)}) async-start(), calls=%async_computation.9 | async-start | bytes 1048576 | tf_op jit(solution)/shard_map/psum | solution.py:9
  937.0 1.2 copy-start.14
  1001.9 95.8 %all-reduce.72.cloned.1.call-start = ((), (), s32[]{:S(2)}) async-start(), calls=%async_computation.19 | async-start | bytes 1048576 | tf_op jit(solution)/shard_map/psum | solution.py:9
  1042.4 111.0 %all-reduce.54.cloned.1.call-start = ((), (), s32[]{:S(2)}) async-start(), calls=%async_computation.10 | async-start | bytes 524288 | tf_op jit(solution)/shard_map/psum | solution.py:9
  1042.6 55.0 %copy-start.2 = (f32[2,256,256]{2,1,0:T(8,128)S(1)}, f32[2,256,256]{2,1,0:T(8,128)}, u32[]{:S(2)}) copy-start(f32[2,256,256]{2,1,0:T(8,128)} %all-reduce.52.cloned.1.call-done) | copy-start | bytes 1572868
  1097.7 1.0 copy-start.17
  1099.5 156.4 %all-reduce.56.cloned.1.call-start = ((), (), s32[]{:S(2)}) async-start(), calls=%async_computation.11 | async-start | bytes 1048576 | tf_op jit(solution)/shard_map/psum | solution.py:9
  1153.4 1.2 copy-start.15
  1218.1 95.8 %all-reduce.70.cloned.1.call-start = ((), (), s32[]{:S(2)}) async-start(), calls=%async_computation.18 | async-start | bytes 1048576 | tf_op jit(solution)/shard_map/psum | solution.py:9
  1258.7 111.1 %all-reduce.58.cloned.1.call-start = ((), (), s32[]{:S(2)}) async-start(), calls=%async_computation.12 | async-start | bytes 524288 | tf_op jit(solution)/shard_map/psum | solution.py:9
  1258.9 55.0 %copy-start.3 = (f32[2,256,256]{2,1,0:T(8,128)S(1)}, f32[2,256,256]{2,1,0:T(8,128)}, u32[]{:S(2)}) copy-start(f32[2,256,256]{2,1,0:T(8,128)} %all-reduce.56.cloned.1.call-done) | copy-start | bytes 1572868
  1314.0 1.0 copy-start.18
  1315.9 156.6 %all-reduce.60.cloned.1.call-start = ((), (), s32[]{:S(2)}) async-start(), calls=%async_computation.13 | async-start | bytes 1048576 | tf_op jit(solution)/shard_map/psum | solution.py:9
  1369.8 1.2 copy-start.16
  1434.7 96.0 %all-reduce.68.cloned.1.call-start = ((), (), s32[]{:S(2)}) async-start(), calls=%async_computation.17 | async-start | bytes 1048576 | tf_op jit(solution)/shard_map/psum | solution.py:9
  1475.3 111.3 %all-reduce.62.cloned.1.call-start = ((), (), s32[]{:S(2)}) async-start(), calls=%async_computation.14 | async-start | bytes 524288 | tf_op jit(solution)/shard_map/psum | solution.py:9
  1475.5 55.2 %copy-start.4 = (f32[2,256,256]{2,1,0:T(8,128)S(1)}, f32[2,256,256]{2,1,0:T(8,128)}, u32[]{:S(2)}) copy-start(f32[2,256,256]{2,1,0:T(8,128)} %all-reduce.60.cloned.1.call-done) | copy-start | bytes 1572868
  1530.7 1.0 copy-start.19
  1532.5 157.0 %all-reduce.64.cloned.1.call-start = ((), (), s32[]{:S(2)}) async-start(), calls=%async_computation.15 | async-start | bytes 1048576 | tf_op jit(solution)/shard_map/psum | solution.py:9
  1587.5 1.0 copy-start.9
  1651.7 95.8 %all-reduce.66.cloned.1.call-start = ((), (), s32[]{:S(2)}) async-start(), calls=%async_computation.16 | async-start | bytes 1048576 | tf_op jit(solution)/shard_map/psum | solution.py:9
  1692.4 55.1 %copy-start.1 = (f32[2,256,256]{2,1,0:T(8,128)S(1)}, f32[2,256,256]{2,1,0:T(8,128)}, u32[]{:S(2)}) copy-start(f32[2,256,256]{2,1,0:T(8,128)} %all-reduce.64.cloned.1.call-done) | copy-start | bytes 1572868
  1747.5 1.0 copy-start.20
Sparse Core Ops, SparseCore 0:
  10.4 56.2 all-reduce.33
  131.2 37.6 all-reduce.35
  172.4 54.6 all-reduce.79
  230.0 54.3 all-reduce.37
  349.3 37.6 all-reduce.39
  390.3 54.6 all-reduce.77
  448.0 54.2 all-reduce.41
  567.4 37.6 all-reduce.43
  608.5 54.6 all-reduce.75
  666.1 54.3 all-reduce.45
  785.4 37.6 all-reduce.47
  826.4 54.6 all-reduce.73
  884.1 52.7 all-reduce.49
  1002.0 37.6 all-reduce.51
  1043.0 54.6 all-reduce.71
  1100.6 52.7 all-reduce.53
  1218.2 37.6 all-reduce.55
  1259.2 54.6 all-reduce.69
  1317.0 52.7 all-reduce.57
  1434.8 37.6 all-reduce.59
  1476.0 54.6 all-reduce.67
  1533.7 52.7 all-reduce.61
  1651.8 37.6 all-reduce.63
  1692.8 54.6 all-reduce.65
where the time goes:
time: 1770 us; the launch traced here: 1760 us
  waiting for transfers between devices  1160 us (66%)
  other arithmetic  477 us (27%)
  local copies, waits for them, and re-layouts  58.3 us (3%)
  between operations  38.5 us (2%)
    psum x24, waiting for transfers between devices, from_root(): return lax.psum(kept, axis)  1160 us
    another operation x55, other arithmetic, shards(): lower_factor = jnp.linalg.cholesky(symmetric)  277 us
    another operation x17, other arithmetic, shards(): jax.scipy.linalg.solve_triangular(lower_factor, flattened.T, lower=True)  158 us
  transfers between devices with their start and end apart: 24, of which 24 were waited for; matrix products, arithmetic and copies ran while one was open for 0% of the time, Pallas kernels for 0%

commit v1 on v0

--- a/solution.py
+++ b/solution.py
@@ -6,7 +6,7 @@
 
 def from_root(value, axis, source):
     kept = jnp.where(lax.axis_index(axis) == source, value, 0).astype(value.dtype)
-    return lax.psum(kept, axis)
+    return jnp.sum(lax.all_gather(kept, axis), axis=0)
 
 
 def pick_tile(tiles, tile_rows, wanted):

time: 1770 us -> 1710 us (0.966)
  waiting for transfers between devices: 1160 us -> 1020 us
  local copies, waits for them, and re-layouts: 58.3 us -> 108 us
  other arithmetic: 477 us -> 522 us
    psum x24 -> x0, waiting for transfers between devices: 1160 us -> none  [from_root(): return lax.psum(kept, axis)]
    all_gather x0 -> x32, waiting for transfers between devices: none -> 1010 us  [from_root(): return jnp.sum(lax.all_gather(kept, axis), axis=0)]
    reduce_sum x0 -> x20, other arithmetic: none -> 25.6 us  [from_root(): return jnp.sum(lax.all_gather(kept, axis), axis=0)]
  transfers between devices with their start and end apart: 24 -> 32, of which waited for: 24 -> 32; matrix products, arithmetic and copies ran while one was open for 0% -> 2% of each run, Pallas kernels for 0% -> 0%
where the time goes in v1:
time: 1710 us; the launch traced here: 1700 us
  waiting for transfers between devices  1020 us (60%)
  other arithmetic  522 us (31%)
  local copies, waits for them, and re-layouts  108 us (6%)
  between operations  37.7 us (2%)
    all_gather x32, waiting for transfers between devices, from_root(): return jnp.sum(lax.all_gather(kept, axis), axis=0)  1010 us
    another operation x55, other arithmetic, shards(): lower_factor = jnp.linalg.cholesky(symmetric)  279 us
    another operation x17, other arithmetic, shards(): jax.scipy.linalg.solve_triangular(lower_factor, flattened.T, lower=True)  158 us
  transfers between devices with their start and end apart: 32, of which 32 were waited for; matrix products, arithmetic and copies ran while one was open for 2% of the time, Pallas kernels for 0%

profile of v1, /device:TPU:0, one launch (start us, length us, event | category | flops | bytes accessed | tf_op | source)
XLA Modules:
  0.0 1702.9 jit_solution(11273299532167243053)
XLA Ops:
  12.7 30.7 %all-gather.73.cloned.1.call-done = f32[2048,256]{0,1:T(8,128)} async-done(((f32[256,256]{0,1:T(8,128)}), f32[2048,256]{0,1:T(8,128)}) %all-gather.73.cloned.1.call-update) | async-done | bytes 2097168 | tf_op jit(solution)/shard_map/all_gather | solution.py:9
  46.9 11.7 cholesky.382
  58.7 9.8 custom-call.25
  68.9 11.7 cholesky.399
  87.3 19.7 %custom-call.26 = f32[2,128,128]{1,2,0:T(8,128)S(1)} custom-call(f32[2,128,128]{2,1,0:T(8,128)S(1)} %get-tuple-element.681), custom_call_target="InvertDiagBlocksLowerTriangular" | custom-call | tf_op jit(solution)/shard_map/jit(_solve_triangular)/triangular_solve | solution.py:43
  111.9 43.6 %all-gather.57.cloned.1.call-done = f32[4,2,256,256]{3,2,1,0:T(8,128)} async-done(((f32[1,2,256,256]{3,2,1,0:T(8,128)}), f32[4,2,256,256]{3,2,1,0:T(8,128)}) %all-gather.57.cloned.1.call-update) | async-done | bytes 2097168 | tf_op jit(solution)/shard_map/all_gather | solution.py:9
  166.2 20.6 %all-gather.75.cloned.1.call-done = f32[2048,256]{0,1:T(8,128)} async-done(((f32[256,256]{0,1:T(8,128)}), f32[2048,256]{0,1:T(8,128)}) %all-gather.75.cloned.1.call-update) | async-done | bytes 2097168 | tf_op jit(solution)/shard_map/all_gather | solution.py:9
  187.9 28.8 %all-gather.77.cloned.1.call-done = f32[2048,256]{0,1:T(8,128)} async-done(((f32[256,256]{0,1:T(8,128)}), f32[2048,256]{0,1:T(8,128)}) %all-gather.77.cloned.1.call-update) | async-done | bytes 2097168 | tf_op jit(solution)/shard_map/all_gather | solution.py:9
  226.7 27.9 %all-gather.79.cloned.1.call-done = f32[2048,256]{0,1:T(8,128)} async-done(((f32[256,256]{0,1:T(8,128)}), f32[2048,256]{0,1:T(8,128)}) %all-gather.79.cloned.1.call-update) | async-done | bytes 2097168 | tf_op jit(solution)/shard_map/all_gather | solution.py:9
  258.0 11.7 cholesky.416
  269.8 9.8 custom-call.27
  280.1 11.7 cholesky.433
  299.1 19.7 %custom-call.28 = f32[2,128,128]{1,2,0:T(8,128)S(1)} custom-call(f32[2,128,128]{2,1,0:T(8,128)S(1)} %get-tuple-element.682), custom_call_target="InvertDiagBlocksLowerTriangular" | custom-call | tf_op jit(solution)/shard_map/jit(_solve_triangular)/triangular_solve | solution.py:43
  321.3 46.0 %all-gather.59.cloned.1.call-done = f32[4,2,256,256]{3,2,1,0:T(8,128)} async-done(((f32[1,2,256,256]{3,2,1,0:T(8,128)}), f32[4,2,256,256]{3,2,1,0:T(8,128)}) %all-gather.59.cloned.1.call-update) | async-done | bytes 2097168 | tf_op jit(solution)/shard_map/all_gather | solution.py:9
  377.3 21.3 %all-gather.81.cloned.1.call-done = f32[2048,256]{0,1:T(8,128)} async-done(((f32[256,256]{0,1:T(8,128)}), f32[2048,256]{0,1:T(8,128)}) %all-gather.81.cloned.1.call-update) | async-done | bytes 2097168 | tf_op jit(solution)/shard_map/all_gather | solution.py:9
  399.7 29.0 %all-gather.83.cloned.1.call-done = f32[2048,256]{0,1:T(8,128)} async-done(((f32[256,256]{0,1:T(8,128)}), f32[2048,256]{0,1:T(8,128)}) %all-gather.83.cloned.1.call-update) | async-done | bytes 2097168 | tf_op jit(solution)/shard_map/all_gather | solution.py:9
  438.6 27.9 %all-gather.85.cloned.1.call-done = f32[2048,256]{0,1:T(8,128)} async-done(((f32[256,256]{0,1:T(8,128)}), f32[2048,256]{0,1:T(8,128)}) %all-gather.85.cloned.1.call-update) | async-done | bytes 2097168 | tf_op jit(solution)/shard_map/all_gather | solution.py:9
  469.9 11.7 cholesky.450
  481.7 9.8 custom-call.29
  492.0 11.7 cholesky.467
  511.0 19.7 %custom-call.30 = f32[2,128,128]{1,2,0:T(8,128)S(1)} custom-call(f32[2,128,128]{2,1,0:T(8,128)S(1)} %get-tuple-element.683), custom_call_target="InvertDiagBlocksLowerTriangular" | custom-call | tf_op jit(solution)/shard_map/jit(_solve_triangular)/triangular_solve | solution.py:43
  533.2 46.0 %all-gather.61.cloned.1.call-done = f32[4,2,256,256]{3,2,1,0:T(8,128)} async-done(((f32[1,2,256,256]{3,2,1,0:T(8,128)}), f32[4,2,256,256]{3,2,1,0:T(8,128)}) %all-gather.61.cloned.1.call-update) | async-done | bytes 2097168 | tf_op jit(solution)/shard_map/all_gather | solution.py:9
  589.2 21.3 %all-gather.87.cloned.1.call-done = f32[2048,256]{0,1:T(8,128)} async-done(((f32[256,256]{0,1:T(8,128)}), f32[2048,256]{0,1:T(8,128)}) %all-gather.87.cloned.1.call-update) | async-done | bytes 2097168 | tf_op jit(solution)/shard_map/all_gather | solution.py:9
  611.6 28.8 %all-gather.89.cloned.1.call-done = f32[2048,256]{0,1:T(8,128)} async-done(((f32[256,256]{0,1:T(8,128)}), f32[2048,256]{0,1:T(8,128)}) %all-gather.89.cloned.1.call-update) | async-done | bytes 2097168 | tf_op jit(solution)/shard_map/all_gather | solution.py:9
  650.3 27.9 %all-gather.91.cloned.1.call-done = f32[2048,256]{0,1:T(8,128)} async-done(((f32[256,256]{0,1:T(8,128)}), f32[2048,256]{0,1:T(8,128)}) %all-gather.91.cloned.1.call-update) | async-done | bytes 2097168 | tf_op jit(solution)/shard_map/all_gather | solution.py:9
  681.7 11.7 cholesky.484
  693.4 9.8 custom-call.31
  703.7 11.7 cholesky.501
  722.7 19.7 %custom-call.32 = f32[2,128,128]{1,2,0:T(8,128)S(1)} custom-call(f32[2,128,128]{2,1,0:T(8,128)S(1)} %get-tuple-element.684), custom_call_target="InvertDiagBlocksLowerTriangular" | custom-call | tf_op jit(solution)/shard_map/jit(_solve_triangular)/triangular_solve | solution.py:43
  744.9 46.0 %all-gather.63.cloned.1.call-done = f32[4,2,256,256]{3,2,1,0:T(8,128)} async-done(((f32[1,2,256,256]{3,2,1,0:T(8,128)}), f32[4,2,256,256]{3,2,1,0:T(8,128)}) %all-gather.63.cloned.1.call-update) | async-done | bytes 2097168 | tf_op jit(solution)/shard_map/all_gather | solution.py:9
  800.9 21.3 %all-gather.93.cloned.1.call-done = f32[2048,256]{0,1:T(8,128)} async-done(((f32[256,256]{0,1:T(8,128)}), f32[2048,256]{0,1:T(8,128)}) %all-gather.93.cloned.1.call-update) | async-done | bytes 2097168 | tf_op jit(solution)/shard_map/all_gather | solution.py:9
  823.3 28.8 %all-gather.95.cloned.1.call-done = f32[2048,256]{0,1:T(8,128)} async-done(((f32[256,256]{0,1:T(8,128)}), f32[2048,256]{0,1:T(8,128)}) %all-gather.95.cloned.1.call-update) | async-done | bytes 2097168 | tf_op jit(solution)/shard_map/all_gather | solution.py:9
  860.1 27.7 %all-gather.97.cloned.1.call-done = f32[2048,256]{0,1:T(8,128)} async-done(((f32[256,256]{0,1:T(8,128)}), f32[2048,256]{0,1:T(8,128)}) %all-gather.97.cloned.1.call-update) | async-done | bytes 2097168 | tf_op jit(solution)/shard_map/all_gather | solution.py:9
  891.2 11.7 cholesky.518
  903.0 9.8 custom-call.33
  913.3 12.1 cholesky.535
  932.3 19.7 %custom-call.34 = f32[2,128,128]{1,2,0:T(8,128)S(1)} custom-call(f32[2,128,128]{2,1,0:T(8,128)S(1)} %get-tuple-element.685), custom_call_target="InvertDiagBlocksLowerTriangular" | custom-call | tf_op jit(solution)/shard_map/jit(_solve_triangular)/triangular_solve | solution.py:43
  954.5 46.0 %all-gather.65.cloned.1.call-done = f32[4,2,256,256]{3,2,1,0:T(8,128)} async-done(((f32[1,2,256,256]{3,2,1,0:T(8,128)}), f32[4,2,256,256]{3,2,1,0:T(8,128)}) %all-gather.65.cloned.1.call-update) | async-done | bytes 2097168 | tf_op jit(solution)/shard_map/all_gather | solution.py:9
  1008.8 22.9 %all-gather.99.cloned.1.call-done = f32[2048,256]{0,1:T(8,128)} async-done(((f32[256,256]{0,1:T(8,128)}), f32[2048,256]{0,1:T(8,128)}) %all-gather.99.cloned.1.call-update) | async-done | bytes 2097168 | tf_op jit(solution)/shard_map/all_gather | solution.py:9
  1032.9 28.9 %all-gather.101.cloned.1.call-done = f32[2048,256]{0,1:T(8,128)} async-done(((f32[256,256]{0,1:T(8,128)}), f32[2048,256]{0,1:T(8,128)}) %all-gather.101.cloned.1.call-update) | async-done | bytes 2097168 | tf_op jit(solution)/shard_map/all_gather | solution.py:9
  1064.1 33.2 %all-gather.103.cloned.1.call-done = f32[2048,256]{0,1:T(8,128)} async-done(((f32[256,256]{0,1:T(8,128)}), f32[2048,256]{0,1:T(8,128)}) %all-gather.103.cloned.1.call-update) | async-done | bytes 2097168 | tf_op jit(solution)/shard_map/all_gather | solution.py:9
  1100.8 11.7 cholesky.552
  1112.5 9.8 custom-call.35
  1122.8 12.1 cholesky.569
  1141.8 19.7 %custom-call.36 = f32[2,128,128]{1,2,0:T(8,128)S(1)} custom-call(f32[2,128,128]{2,1,0:T(8,128)S(1)} %get-tuple-element.686), custom_call_target="InvertDiagBlocksLowerTriangular" | custom-call | tf_op jit(solution)/shard_map/jit(_solve_triangular)/triangular_solve | solution.py:43
  1164.0 46.0 %all-gather.67.cloned.1.call-done = f32[4,2,256,256]{3,2,1,0:T(8,128)} async-done(((f32[1,2,256,256]{3,2,1,0:T(8,128)}), f32[4,2,256,256]{3,2,1,0:T(8,128)}) %all-gather.67.cloned.1.call-update) | async-done | bytes 2097168 | tf_op jit(solution)/shard_map/all_gather | solution.py:9
  1218.4 22.9 %all-gather.105.cloned.1.call-done = f32[2048,256]{0,1:T(8,128)} async-done(((f32[256,256]{0,1:T(8,128)}), f32[2048,256]{0,1:T(8,128)}) %all-gather.105.cloned.1.call-update) | async-done | bytes 2097168 | tf_op jit(solution)/shard_map/all_gather | solution.py:9
  1242.4 28.9 %all-gather.107.cloned.1.call-done = f32[2048,256]{0,1:T(8,128)} async-done(((f32[256,256]{0,1:T(8,128)}), f32[2048,256]{0,1:T(8,128)}) %all-gather.107.cloned.1.call-update) | async-done | bytes 2097168 | tf_op jit(solution)/shard_map/all_gather | solution.py:9
  1273.7 33.2 %all-gather.109.cloned.1.call-done = f32[2048,256]{0,1:T(8,128)} async-done(((f32[256,256]{0,1:T(8,128)}), f32[2048,256]{0,1:T(8,128)}) %all-gather.109.cloned.1.call-update) | async-done | bytes 2097168 | tf_op jit(solution)/shard_map/all_gather | solution.py:9
  1310.3 11.7 cholesky.586
  1322.1 9.8 custom-call.37
  1332.4 12.1 cholesky.603
  1351.4 19.7 %custom-call.38 = f32[2,128,128]{1,2,0:T(8,128)S(1)} custom-call(f32[2,128,128]{2,1,0:T(8,128)S(1)} %get-tuple-element.687), custom_call_target="InvertDiagBlocksLowerTriangular" | custom-call | tf_op jit(solution)/shard_map/jit(_solve_triangular)/triangular_solve | solution.py:43
  1373.6 46.0 %all-gather.69.cloned.1.call-done = f32[4,2,256,256]{3,2,1,0:T(8,128)} async-done(((f32[1,2,256,256]{3,2,1,0:T(8,128)}), f32[4,2,256,256]{3,2,1,0:T(8,128)}) %all-gather.69.cloned.1.call-update) | async-done | bytes 2097168 | tf_op jit(solution)/shard_map/all_gather | solution.py:9
  1428.0 22.9 %all-gather.111.cloned.1.call-done = f32[2048,256]{0,1:T(8,128)} async-done(((f32[256,256]{0,1:T(8,128)}), f32[2048,256]{0,1:T(8,128)}) %all-gather.111.cloned.1.call-update) | async-done | bytes 2097168 | tf_op jit(solution)/shard_map/all_gather | solution.py:9
  1452.0 29.0 %all-gather.113.cloned.1.call-done = f32[2048,256]{0,1:T(8,128)} async-done(((f32[256,256]{0,1:T(8,128)}), f32[2048,256]{0,1:T(8,128)}) %all-gather.113.cloned.1.call-update) | async-done | bytes 2097168 | tf_op jit(solution)/shard_map/all_gather | solution.py:9
  1483.4 33.2 %all-gather.115.cloned.1.call-done = f32[2048,256]{0,1:T(8,128)} async-done(((f32[256,256]{0,1:T(8,128)}), f32[2048,256]{0,1:T(8,128)}) %all-gather.115.cloned.1.call-update) | async-done | bytes 2097168 | tf_op jit(solution)/shard_map/all_gather | solution.py:9
  1520.0 11.7 cholesky.620
  1531.8 9.8 custom-call.39
  1542.1 11.9 cholesky.637
  1560.9 19.7 %custom-call.40 = f32[2,128,128]{1,2,0:T(8,128)S(1)} custom-call(f32[2,128,128]{2,1,0:T(8,128)S(1)} %get-tuple-element.688), custom_call_target="InvertDiagBlocksLowerTriangular" | custom-call | tf_op jit(solution)/shard_map/jit(_solve_triangular)/triangular_solve | solution.py:43
  1583.1 46.0 %all-gather.71.cloned.1.call-done = f32[4,2,256,256]{3,2,1,0:T(8,128)} async-done(((f32[1,2,256,256]{3,2,1,0:T(8,128)}), f32[4,2,256,256]{3,2,1,0:T(8,128)}) %all-gather.71.cloned.1.call-update) | async-done | bytes 2097168 | tf_op jit(solution)/shard_map/all_gather | solution.py:9
  1637.4 23.0 %all-gather.117.cloned.1.call-done = f32[2048,256]{0,1:T(8,128)} async-done(((f32[256,256]{0,1:T(8,128)}), f32[2048,256]{0,1:T(8,128)}) %all-gather.117.cloned.1.call-update) | async-done | bytes 2097168 | tf_op jit(solution)/shard_map/all_gather | solution.py:9
  1661.5 29.0 %all-gather.119.cloned.1.call-done = f32[2048,256]{0,1:T(8,128)} async-done(((f32[256,256]{0,1:T(8,128)}), f32[2048,256]{0,1:T(8,128)}) %all-gather.119.cloned.1.call-update) | async-done | bytes 2097168 | tf_op jit(solution)/shard_map/all_gather | solution.py:9
  (532 shorter events, 288.2 us)
Async XLA Ops:
  6.5 3.3 copy-start
  6.5 36.9 %all-gather.73.cloned.1.call-start = ((), (), s32[]{:S(2)}) async-start(), calls=%async_computation.8 | async-start | bytes 2359296 | tf_op jit(solution)/shard_map/all_gather | solution.py:9
  12.4 143.2 %all-gather.57.cloned.1.call-start = ((), (), s32[]{:S(2)}) async-start(), calls=%async_computation | async-start | bytes 2621440 | tf_op jit(solution)/shard_map/all_gather | solution.py:9
  109.5 77.3 %all-gather.75.cloned.1.call-start = ((), (), s32[]{:S(2)}) async-start(), calls=%async_computation.9 | async-start | bytes 2359296 | tf_op jit(solution)/shard_map/all_gather | solution.py:9
  159.7 57.0 %all-gather.77.cloned.1.call-start = ((), (), s32[]{:S(2)}) async-start(), calls=%async_computation.10 | async-start | bytes 2359296 | tf_op jit(solution)/shard_map/all_gather | solution.py:9
  161.2 93.4 %all-gather.79.cloned.1.call-start = ((), (), s32[]{:S(2)}) async-start(), calls=%async_computation.11 | async-start | bytes 2359296 | tf_op jit(solution)/shard_map/all_gather | solution.py:9
  226.2 141.1 %all-gather.59.cloned.1.call-start = ((), (), s32[]{:S(2)}) async-start(), calls=%async_computation.1 | async-start | bytes 2621440 | tf_op jit(solution)/shard_map/all_gather | solution.py:9
  321.2 77.3 %all-gather.81.cloned.1.call-start = ((), (), s32[]{:S(2)}) async-start(), calls=%async_computation.12 | async-start | bytes 2359296 | tf_op jit(solution)/shard_map/all_gather | solution.py:9
  371.5 57.2 %all-gather.83.cloned.1.call-start = ((), (), s32[]{:S(2)}) async-start(), calls=%async_computation.13 | async-start | bytes 2359296 | tf_op jit(solution)/shard_map/all_gather | solution.py:9
  372.3 94.2 %all-gather.85.cloned.1.call-start = ((), (), s32[]{:S(2)}) async-start(), calls=%async_computation.14 | async-start | bytes 2359296 | tf_op jit(solution)/shard_map/all_gather | solution.py:9
  438.1 141.1 %all-gather.61.cloned.1.call-start = ((), (), s32[]{:S(2)}) async-start(), calls=%async_computation.2 | async-start | bytes 2621440 | tf_op jit(solution)/shard_map/all_gather | solution.py:9
  533.1 77.3 %all-gather.87.cloned.1.call-start = ((), (), s32[]{:S(2)}) async-start(), calls=%async_computation.15 | async-start | bytes 2359296 | tf_op jit(solution)/shard_map/all_gather | solution.py:9
  583.4 57.1 %all-gather.89.cloned.1.call-start = ((), (), s32[]{:S(2)}) async-start(), calls=%async_computation.16 | async-start | bytes 2359296 | tf_op jit(solution)/shard_map/all_gather | solution.py:9
  584.2 94.1 %all-gather.91.cloned.1.call-start = ((), (), s32[]{:S(2)}) async-start(), calls=%async_computation.17 | async-start | bytes 2359296 | tf_op jit(solution)/shard_map/all_gather | solution.py:9
  649.9 141.1 %all-gather.63.cloned.1.call-start = ((), (), s32[]{:S(2)}) async-start(), calls=%async_computation.3 | async-start | bytes 2621440 | tf_op jit(solution)/shard_map/all_gather | solution.py:9
  744.9 77.3 %all-gather.93.cloned.1.call-start = ((), (), s32[]{:S(2)}) async-start(), calls=%async_computation.18 | async-start | bytes 2359296 | tf_op jit(solution)/shard_map/all_gather | solution.py:9
  795.1 57.0 %all-gather.95.cloned.1.call-start = ((), (), s32[]{:S(2)}) async-start(), calls=%async_computation.19 | async-start | bytes 2359296 | tf_op jit(solution)/shard_map/all_gather | solution.py:9
  795.9 91.8 %all-gather.97.cloned.1.call-start = ((), (), s32[]{:S(2)}) async-start(), calls=%async_computation.20 | async-start | bytes 2359296 | tf_op jit(solution)/shard_map/all_gather | solution.py:9
  859.4 141.1 %all-gather.65.cloned.1.call-start = ((), (), s32[]{:S(2)}) async-start(), calls=%async_computation.4 | async-start | bytes 2621440 | tf_op jit(solution)/shard_map/all_gather | solution.py:9
  954.4 77.4 %all-gather.99.cloned.1.call-start = ((), (), s32[]{:S(2)}) async-start(), calls=%async_computation.21 | async-start | bytes 2359296 | tf_op jit(solution)/shard_map/all_gather | solution.py:9
  1004.7 57.0 %all-gather.101.cloned.1.call-start = ((), (), s32[]{:S(2)}) async-start(), calls=%async_computation.22 | async-start | bytes 2359296 | tf_op jit(solution)/shard_map/all_gather | solution.py:9
  1005.5 91.8 %all-gather.103.cloned.1.call-start = ((), (), s32[]{:S(2)}) async-start(), calls=%async_computation.23 | async-start | bytes 2359296 | tf_op jit(solution)/shard_map/all_gather | solution.py:9
  1063.5 146.5 %all-gather.67.cloned.1.call-start = ((), (), s32[]{:S(2)}) async-start(), calls=%async_computation.5 | async-start | bytes 2621440 | tf_op jit(solution)/shard_map/all_gather | solution.py:9
  1164.0 77.4 %all-gather.105.cloned.1.call-start = ((), (), s32[]{:S(2)}) async-start(), calls=%async_computation.24 | async-start | bytes 2359296 | tf_op jit(solution)/shard_map/all_gather | solution.py:9
  1214.2 57.1 %all-gather.107.cloned.1.call-start = ((), (), s32[]{:S(2)}) async-start(), calls=%async_computation.25 | async-start | bytes 2359296 | tf_op jit(solution)/shard_map/all_gather | solution.py:9
  1215.0 91.9 %all-gather.109.cloned.1.call-start = ((), (), s32[]{:S(2)}) async-start(), calls=%async_computation.26 | async-start | bytes 2359296 | tf_op jit(solution)/shard_map/all_gather | solution.py:9
  1273.1 146.5 %all-gather.69.cloned.1.call-start = ((), (), s32[]{:S(2)}) async-start(), calls=%async_computation.6 | async-start | bytes 2621440 | tf_op jit(solution)/shard_map/all_gather | solution.py:9
  1373.5 77.4 %all-gather.111.cloned.1.call-start = ((), (), s32[]{:S(2)}) async-start(), calls=%async_computation.27 | async-start | bytes 2359296 | tf_op jit(solution)/shard_map/all_gather | solution.py:9
  1423.8 57.2 %all-gather.113.cloned.1.call-start = ((), (), s32[]{:S(2)}) async-start(), calls=%async_computation.28 | async-start | bytes 2359296 | tf_op jit(solution)/shard_map/all_gather | solution.py:9
  1424.6 92.0 %all-gather.115.cloned.1.call-start = ((), (), s32[]{:S(2)}) async-start(), calls=%async_computation.29 | async-start | bytes 2359296 | tf_op jit(solution)/shard_map/all_gather | solution.py:9
  1482.8 146.4 %all-gather.71.cloned.1.call-start = ((), (), s32[]{:S(2)}) async-start(), calls=%async_computation.7 | async-start | bytes 2621440 | tf_op jit(solution)/shard_map/all_gather | solution.py:9
  1583.0 77.3 %all-gather.117.cloned.1.call-start = ((), (), s32[]{:S(2)}) async-start(), calls=%async_computation.30 | async-start | bytes 2359296 | tf_op jit(solution)/shard_map/all_gather | solution.py:9
  1633.3 57.2 %all-gather.119.cloned.1.call-start = ((), (), s32[]{:S(2)}) async-start(), calls=%async_computation.31 | async-start | bytes 2359296 | tf_op jit(solution)/shard_map/all_gather | solution.py:9
Sparse Core Ops, SparseCore 0:
  12.5 30.8 all-gather.72
  109.6 45.9 all-gather.56
  159.8 26.8 all-gather.74
  188.5 28.1 all-gather.76
  226.3 28.1 all-gather.78
  321.3 45.9 all-gather.58
  371.6 26.9 all-gather.80
  400.4 28.1 all-gather.82
  438.2 28.1 all-gather.84
  533.2 45.9 all-gather.60
  583.5 26.9 all-gather.86
  612.2 28.1 all-gather.88
  650.0 28.1 all-gather.90
  745.0 45.9 all-gather.62
  795.2 26.9 all-gather.92
  823.9 28.1 all-gather.94
  859.5 28.1 all-gather.96
  954.5 45.9 all-gather.64
  1004.8 26.9 all-gather.98
  1033.5 28.1 all-gather.100
  1063.6 33.6 all-gather.102
  1164.1 45.9 all-gather.66
  1214.3 26.9 all-gather.104
  1243.1 28.1 all-gather.106
  1273.2 33.6 all-gather.108
  1373.6 45.9 all-gather.68
  1423.9 26.9 all-gather.110
  1452.8 28.1 all-gather.112
  1482.9 33.6 all-gather.114
  1583.2 45.9 all-gather.70
  1633.4 26.8 all-gather.116
  1662.3 28.1 all-gather.118
